TPU v7x, 32 devices: a whole 2x2x4 slice. The times are simulated.
32 devices in a mesh: gx: 4 (over z), gy: 4 (over x, core), gz: 2 (over y).
Axes of the slice: x: 2, y: 2, z: 4, core: 2. Of those that a mesh axis runs over, the one named last changes fastest.
Arguments:
- residual: float32 [32, 32, 256], P('gx', 'gy', 'gz'), may hold values from -18 to 18
- direction: float32 [32, 32, 256], P('gx', 'gy', 'gz'), may hold values from -18 to 18
Outputs:
- powers: float32 [2, 4, 32, 32, 256], P(None, None, 'gx', 'gy', 'gz')
- gram_matrix: float32 [9, 9], replicated
- projections: float32 [9], replicated
All inputs are finite; a program needn't handle non-finite values.
Results may differ from a plain program's by a relative error of at most 0.00029.
Values sent between devices are 32-bit elements; how exact they have to be, the bound alone decides.
A program may use at most 64 MiB of HBM per device.

v0:
```python
import jax
import jax.numpy as jnp
from jax import lax
from jax.sharding import PartitionSpec as P

STEPS = 4
MARGIN = 1
SWEEPS = 3
SWEEP_SCALE = 1.0 / 9.0


def extended(cells, sides, width):
    for axis, dim in sides:
        count = lax.axis_size(axis)
        ends = count - 1
        head = lax.slice_in_dim(cells, 0, width, axis=dim)
        tail = lax.slice_in_dim(cells, cells.shape[dim] - width, cells.shape[dim], axis=dim)
        cells = jnp.concatenate(
            [
                lax.ppermute(tail, axis, [(i, (i + 1) % count) for i in range(ends)]),
                cells,
                lax.ppermute(head, axis, [((i + 1) % count, i) for i in range(ends)]),
            ],
            axis=dim,
        )
    return cells


def stencil_image(padded):
    center = padded[:, 1:-1, 1:-1, 1:-1]
    beside = padded[:, 2:, 1:-1, 1:-1] + padded[:, :-2, 1:-1, 1:-1]
    beside = beside + padded[:, 1:-1, 2:, 1:-1] + padded[:, 1:-1, :-2, 1:-1]
    beside = beside + padded[:, 1:-1, 1:-1, 2:] + padded[:, 1:-1, 1:-1, :-2]
    return 6.0 * center - beside


def pad_along(values, dimension, before, after):
    widths = [(0, 0)] * values.ndim
    widths[dimension] = (before, after)
    return jnp.pad(values, widths)


def assemble(received, reach, growth):
    for dimension in (1, 2, 3):
        length = received.shape[dimension] - 2 * reach
        result_len = length + 2 * growth
        middle = lax.slice_in_dim(received, reach, reach + length, axis=dimension)
        middle = pad_along(middle, dimension, growth, growth)
        below_part = lax.slice_in_dim(received, 0, reach, axis=dimension)
        above_part = lax.slice_in_dim(received, reach + length, 2 * reach + length, axis=dimension)
        received = (
            middle
            + pad_along(below_part, dimension, 0, result_len - reach)
            + pad_along(above_part, dimension, result_len - reach, 0)
        )
    return received


def inside_profile(position, cells, devices, margin):
    global_spots = position * cells - margin + jnp.arange(cells + 2 * margin, dtype=jnp.int32)
    return jnp.logical_and(global_spots >= 0, global_spots < devices * cells).astype(jnp.float32)


def grid_mask(cells_x, cells_y, cells_z, margin):
    along_x = inside_profile(lax.axis_index("gx"), cells_x, lax.axis_size("gx"), margin)
    along_y = inside_profile(lax.axis_index("gy"), cells_y, lax.axis_size("gy"), margin)
    along_z = inside_profile(lax.axis_index("gz"), cells_z, lax.axis_size("gz"), margin)
    return along_x[:, None, None] * along_y[None, :, None] * along_z[None, None, :]


def subdomain_solve(source, mask):
    source = mask * source
    iterate = mask * (SWEEP_SCALE * source)
    for sweep_index in range(SWEEPS - 1):
        padded = jnp.pad(iterate, ((0, 0), (1, 1), (1, 1), (1, 1)))
        iterate = mask * (iterate + SWEEP_SCALE * (source - stencil_image(padded)))
    return iterate


def flatten_rows(fields):
    return jnp.stack([member_field.reshape(-1) for member_field in fields])


def inner_table(left_rows, right_rows):
    return jnp.einsum("ac,bc->ab", left_rows, right_rows, precision=lax.Precision.HIGHEST)


def inner_vector(left_rows, target):
    return jnp.einsum("ac,c->a", left_rows, target, precision=lax.Precision.HIGHEST)


def local(residual, direction):
    margin = MARGIN
    cells_x, cells_y, cells_z = residual.shape
    mask = grid_mask(cells_x, cells_y, cells_z, margin)
    cell_count = float(
        lax.axis_size("gx")
        * cells_x
        * lax.axis_size("gy")
        * cells_y
        * lax.axis_size("gz")
        * cells_z
    )
    target = residual.reshape(-1)
    pieces = jnp.pad(
        jnp.stack([direction, residual]),
        ((0, 0), (margin, margin), (margin, margin), (margin, margin)),
    )
    p_fields, p_images, z_fields, z_images = ([], [], [], [])
    for step_index in range(STEPS + 1):
        final_step = step_index == STEPS
        source = None
        deep_reach = 2 * margin + 1
        received = extended(pieces, (("gx", 1), ("gy", 2), ("gz", 3)), deep_reach)
        region = assemble(received, deep_reach, 1)
        fields = region[
            :,
            margin + 1 : margin + 1 + cells_x,
            margin + 1 : margin + 1 + cells_y,
            margin + 1 : margin + 1 + cells_z,
        ]
        if final_step:
            own_images = stencil_image(
                region[
                    :,
                    margin : margin + cells_x + 2,
                    margin : margin + cells_y + 2,
                    margin : margin + cells_z + 2,
                ]
            )
        else:
            wide_images = stencil_image(region)
            own_images = wide_images[
                :, margin : margin + cells_x, margin : margin + cells_y, margin : margin + cells_z
            ]
            if step_index == 0:
                source = jnp.stack([wide_images[0], region[1, 1:-1, 1:-1, 1:-1]])
            else:
                source = wide_images
        p_fields.append(fields[0])
        p_images.append(own_images[0])
        if step_index > 0:
            z_fields.append(fields[1])
            z_images.append(own_images[1])
        if not final_step:
            pieces = subdomain_solve(source, mask)
    basis_rows = flatten_rows(p_fields + z_fields)
    image_rows = flatten_rows(p_images + z_images)
    gram_sum, projection_sum = lax.psum(
        (inner_table(basis_rows, image_rows), inner_vector(basis_rows, target)), ("gx", "gy", "gz")
    )
    powers = jnp.stack([jnp.stack(p_fields[1:]), jnp.stack(z_fields)])
    return (powers, gram_sum / cell_count, projection_sum / cell_count)


def solution(mesh):
    placed = (P("gx", "gy", "gz"), P("gx", "gy", "gz"))
    return jax.shard_map(
        local,
        mesh=mesh,
        in_specs=placed,
        out_specs=(P(None, None, "gx", "gy", "gz"), P(), P()),
        check_vma=False,
    )
```

profile of v0, /device:TPU:14, one launch (start us, length us, event | category | flops | bytes accessed | tf_op | source)
XLA Modules:
  0.0 197.7 jit_solution(4123972771521606894)
XLA Ops:
  1.6 3.5 %collective-permute-start = (f32[2,3,10,130]{3,2,1,0:T(8,128)S(1)}, f32[2,3,10,130]{3,2,1,0:T(8,128)S(1)}, u32[]{:S(2)}, u32[]{:S(2)}) collective-permute-start(f32[2,3,10,130]{3,2,1,0:T(8,128)S(1)} %get-tuple-element.53), channel_id=1, source_target_pairs={{0,8},{8,16},{16,24},{1,9},{9,17},{17,25},{2,10},{10,18},{18,26},{... | collective-permute-start | bytes 93608 | tf_op jit(solution)/shard_map/ppermute | solution.py:20
  5.1 2.4 %collective-permute-start.1 = (f32[2,3,10,130]{3,2,1,0:T(8,128)S(1)}, f32[2,3,10,130]{3,2,1,0:T(8,128)S(1)}, u32[]{:S(2)}, u32[]{:S(2)}) collective-permute-start(f32[2,3,10,130]{3,2,1,0:T(8,128)S(1)} %get-tuple-element.54), channel_id=1, source_target_pairs={{8,0},{16,8},{24,16},{9,1},{17,9},{25,17},{10,2},{18,10},{26,18},{... | collective-permute-start | bytes 93608 | tf_op jit(solution)/shard_map/ppermute | solution.py:22
  8.1 3.5 %collective-permute-done.1 = f32[2,3,10,130]{3,2,1,0:T(8,128)S(1)} collective-permute-done((f32[2,3,10,130]{3,2,1,0:T(8,128)S(1)}, f32[2,3,10,130]{3,2,1,0:T(8,128)S(1)}, u32[]{:S(2)}, u32[]{:S(2)}) %collective-permute-start.1) | collective-permute-done | bytes 31232 | tf_op jit(solution)/shard_map/ppermute | solution.py:22
  13.6 3.6 %collective-permute-start.3 = (f32[2,16,3,130]{3,2,1,0:T(4,128)S(1)}, f32[2,16,3,130]{3,2,1,0:T(4,128)S(1)}, u32[]{:S(2)}, u32[]{:S(2)}) collective-permute-start(f32[2,16,3,130]{3,2,1,0:T(4,128)S(1)} %get-tuple-element.30), channel_id=1, source_target_pairs={{2,0},{4,2},{6,4},{3,1},{5,3},{7,5},{10,8},{12,10},{14,12},{11,9},... | collective-permute-start | bytes 149768 | tf_op jit(solution)/shard_map/ppermute | solution.py:22
  21.3 4.6 %collective-permute-start.5 = (f32[2,16,16,3]{3,2,1,0:T(8,128)S(1)}, f32[2,16,16,3]{3,2,1,0:T(8,128)S(1)}, u32[]{:S(2)}, u32[]{:S(2)}) collective-permute-start(f32[2,16,16,3]{3,2,1,0:T(8,128)S(1)} %get-tuple-element.28), channel_id=1, source_target_pairs={{1,0},{3,2},{5,4},{7,6},{9,8},{11,10},{13,12},{15,14},{17,16},{19,... | collective-permute-start | bytes 18440 | tf_op jit(solution)/shard_map/ppermute | solution.py:22
  26.0 2.3 %collective-permute-done.4 = f32[2,16,16,3]{3,2,1,0:T(8,128)S(1)} collective-permute-done((f32[2,16,16,3]{3,2,1,0:T(8,128)S(1)}, f32[2,16,16,3]{3,2,1,0:T(8,128)S(1)}, u32[]{:S(2)}, u32[]{:S(2)}) %collective-permute-start.4) | collective-permute-done | bytes 6176 | tf_op jit(solution)/shard_map/ppermute | solution.py:20
  33.6 3.5 %collective-permute-start.6 = (f32[2,3,10,130]{3,2,1,0:T(8,128)S(1)}, f32[2,3,10,130]{3,2,1,0:T(8,128)S(1)}, u32[]{:S(2)}, u32[]{:S(2)}) collective-permute-start(f32[2,3,10,130]{3,2,1,0:T(8,128)S(1)} %get-tuple-element.51), channel_id=1, source_target_pairs={{0,8},{8,16},{16,24},{1,9},{9,17},{17,25},{2,10},{10,18},{18,26},{... | collective-permute-start | bytes 93608 | tf_op jit(solution)/shard_map/ppermute | solution.py:20
  37.1 2.4 %collective-permute-start.7 = (f32[2,3,10,130]{3,2,1,0:T(8,128)S(1)}, f32[2,3,10,130]{3,2,1,0:T(8,128)S(1)}, u32[]{:S(2)}, u32[]{:S(2)}) collective-permute-start(f32[2,3,10,130]{3,2,1,0:T(8,128)S(1)} %get-tuple-element.52), channel_id=1, source_target_pairs={{8,0},{16,8},{24,16},{9,1},{17,9},{25,17},{10,2},{18,10},{26,18},{... | collective-permute-start | bytes 93608 | tf_op jit(solution)/shard_map/ppermute | solution.py:22
  40.1 3.5 %collective-permute-done.7 = f32[2,3,10,130]{3,2,1,0:T(8,128)S(1)} collective-permute-done((f32[2,3,10,130]{3,2,1,0:T(8,128)S(1)}, f32[2,3,10,130]{3,2,1,0:T(8,128)S(1)}, u32[]{:S(2)}, u32[]{:S(2)}) %collective-permute-start.7) | collective-permute-done | bytes 31232 | tf_op jit(solution)/shard_map/ppermute | solution.py:22
  45.6 3.6 %collective-permute-start.9 = (f32[2,16,3,130]{3,2,1,0:T(4,128)S(1)}, f32[2,16,3,130]{3,2,1,0:T(4,128)S(1)}, u32[]{:S(2)}, u32[]{:S(2)}) collective-permute-start(f32[2,16,3,130]{3,2,1,0:T(4,128)S(1)} %get-tuple-element.26), channel_id=1, source_target_pairs={{2,0},{4,2},{6,4},{3,1},{5,3},{7,5},{10,8},{12,10},{14,12},{11,9},... | collective-permute-start | bytes 149768 | tf_op jit(solution)/shard_map/ppermute | solution.py:22
  53.3 4.6 %collective-permute-start.11 = (f32[2,16,16,3]{3,2,1,0:T(8,128)S(1)}, f32[2,16,16,3]{3,2,1,0:T(8,128)S(1)}, u32[]{:S(2)}, u32[]{:S(2)}) collective-permute-start(f32[2,16,16,3]{3,2,1,0:T(8,128)S(1)} %get-tuple-element.24), channel_id=1, source_target_pairs={{1,0},{3,2},{5,4},{7,6},{9,8},{11,10},{13,12},{15,14},{17,16},{19,... | collective-permute-start | bytes 18440 | tf_op jit(solution)/shard_map/ppermute | solution.py:22
  57.9 2.4 %collective-permute-done.10 = f32[2,16,16,3]{3,2,1,0:T(8,128)S(1)} collective-permute-done((f32[2,16,16,3]{3,2,1,0:T(8,128)S(1)}, f32[2,16,16,3]{3,2,1,0:T(8,128)S(1)}, u32[]{:S(2)}, u32[]{:S(2)}) %collective-permute-start.10) | collective-permute-done | bytes 6176 | tf_op jit(solution)/shard_map/ppermute | solution.py:20
  66.3 3.9 %collective-permute-start.13 = (f32[2,3,10,130]{3,2,1,0:T(8,128)S(1)}, f32[2,3,10,130]{3,2,1,0:T(8,128)S(1)}, u32[]{:S(2)}, u32[]{:S(2)}) collective-permute-start(f32[2,3,10,130]{3,2,1,0:T(8,128)S(1)} %get-tuple-element.50), channel_id=1, source_target_pairs={{8,0},{16,8},{24,16},{9,1},{17,9},{25,17},{10,2},{18,10},{26,18},{... | collective-permute-start | bytes 93608 | tf_op jit(solution)/shard_map/ppermute | solution.py:22
  74.8 3.6 %collective-permute-start.15 = (f32[2,16,3,130]{3,2,1,0:T(4,128)S(1)}, f32[2,16,3,130]{3,2,1,0:T(4,128)S(1)}, u32[]{:S(2)}, u32[]{:S(2)}) collective-permute-start(f32[2,16,3,130]{3,2,1,0:T(4,128)S(1)} %get-tuple-element.22), channel_id=1, source_target_pairs={{2,0},{4,2},{6,4},{3,1},{5,3},{7,5},{10,8},{12,10},{14,12},{11,9},... | collective-permute-start | bytes 149768 | tf_op jit(solution)/shard_map/ppermute | solution.py:22
  82.5 4.6 %collective-permute-start.17 = (f32[2,16,16,3]{3,2,1,0:T(8,128)S(1)}, f32[2,16,16,3]{3,2,1,0:T(8,128)S(1)}, u32[]{:S(2)}, u32[]{:S(2)}) collective-permute-start(f32[2,16,16,3]{3,2,1,0:T(8,128)S(1)} %get-tuple-element.20), channel_id=1, source_target_pairs={{1,0},{3,2},{5,4},{7,6},{9,8},{11,10},{13,12},{15,14},{17,16},{19,... | collective-permute-start | bytes 18440 | tf_op jit(solution)/shard_map/ppermute | solution.py:22
  87.2 2.2 %collective-permute-done.16 = f32[2,16,16,3]{3,2,1,0:T(8,128)S(1)} collective-permute-done((f32[2,16,16,3]{3,2,1,0:T(8,128)S(1)}, f32[2,16,16,3]{3,2,1,0:T(8,128)S(1)}, u32[]{:S(2)}, u32[]{:S(2)}) %collective-permute-start.16) | collective-permute-done | bytes 6176 | tf_op jit(solution)/shard_map/ppermute | solution.py:20
  95.4 3.9 %collective-permute-start.19 = (f32[2,3,10,130]{3,2,1,0:T(8,128)S(1)}, f32[2,3,10,130]{3,2,1,0:T(8,128)S(1)}, u32[]{:S(2)}, u32[]{:S(2)}) collective-permute-start(f32[2,3,10,130]{3,2,1,0:T(8,128)S(1)} %get-tuple-element.48), channel_id=1, source_target_pairs={{8,0},{16,8},{24,16},{9,1},{17,9},{25,17},{10,2},{18,10},{26,18},{... | collective-permute-start | bytes 93608 | tf_op jit(solution)/shard_map/ppermute | solution.py:22
  103.9 3.6 %collective-permute-start.21 = (f32[2,16,3,130]{3,2,1,0:T(4,128)S(1)}, f32[2,16,3,130]{3,2,1,0:T(4,128)S(1)}, u32[]{:S(2)}, u32[]{:S(2)}) collective-permute-start(f32[2,16,3,130]{3,2,1,0:T(4,128)S(1)} %get-tuple-element.18), channel_id=1, source_target_pairs={{2,0},{4,2},{6,4},{3,1},{5,3},{7,5},{10,8},{12,10},{14,12},{11,9},... | collective-permute-start | bytes 149768 | tf_op jit(solution)/shard_map/ppermute | solution.py:22
  111.6 4.8 %collective-permute-start.23 = (f32[2,16,16,3]{3,2,1,0:T(8,128)S(1)}, f32[2,16,16,3]{3,2,1,0:T(8,128)S(1)}, u32[]{:S(2)}, u32[]{:S(2)}) collective-permute-start(f32[2,16,16,3]{3,2,1,0:T(8,128)S(1)} %get-tuple-element.16), channel_id=1, source_target_pairs={{1,0},{3,2},{5,4},{7,6},{9,8},{11,10},{13,12},{15,14},{17,16},{19,... | collective-permute-start | bytes 18440 | tf_op jit(solution)/shard_map/ppermute | solution.py:22
  124.6 3.9 %collective-permute-start.25 = (f32[2,3,10,130]{3,2,1,0:T(8,128)S(1)}, f32[2,3,10,130]{3,2,1,0:T(8,128)S(1)}, u32[]{:S(2)}, u32[]{:S(2)}) collective-permute-start(f32[2,3,10,130]{3,2,1,0:T(8,128)S(1)} %get-tuple-element.46), channel_id=1, source_target_pairs={{8,0},{16,8},{24,16},{9,1},{17,9},{25,17},{10,2},{18,10},{26,18},{... | collective-permute-start | bytes 93608 | tf_op jit(solution)/shard_map/ppermute | solution.py:22
  133.1 3.6 %collective-permute-start.27 = (f32[2,16,3,130]{3,2,1,0:T(4,128)S(1)}, f32[2,16,3,130]{3,2,1,0:T(4,128)S(1)}, u32[]{:S(2)}, u32[]{:S(2)}) collective-permute-start(f32[2,16,3,130]{3,2,1,0:T(4,128)S(1)} %get-tuple-element.14), channel_id=1, source_target_pairs={{2,0},{4,2},{6,4},{3,1},{5,3},{7,5},{10,8},{12,10},{14,12},{11,9},... | collective-permute-start | bytes 149768 | tf_op jit(solution)/shard_map/ppermute | solution.py:22
  140.8 4.6 %collective-permute-start.29 = (f32[2,16,16,3]{3,2,1,0:T(8,128)S(1)}, f32[2,16,16,3]{3,2,1,0:T(8,128)S(1)}, u32[]{:S(2)}, u32[]{:S(2)}) collective-permute-start(f32[2,16,16,3]{3,2,1,0:T(8,128)S(1)} %get-tuple-element.12), channel_id=1, source_target_pairs={{1,0},{3,2},{5,4},{7,6},{9,8},{11,10},{13,12},{15,14},{17,16},{19,... | collective-permute-start | bytes 18440 | tf_op jit(solution)/shard_map/ppermute | solution.py:22
  145.5 2.3 %collective-permute-done.28 = f32[2,16,16,3]{3,2,1,0:T(8,128)S(1)} collective-permute-done((f32[2,16,16,3]{3,2,1,0:T(8,128)S(1)}, f32[2,16,16,3]{3,2,1,0:T(8,128)S(1)}, u32[]{:S(2)}, u32[]{:S(2)}) %collective-permute-start.28) | collective-permute-done | bytes 6176 | tf_op jit(solution)/shard_map/ppermute | solution.py:20
  153.3 42.5 %all-reduce.39 = (f32[9,9]{1,0:T(8,128)S(1)}, f32[9]{0:T(128)S(1)}) all-reduce(f32[9,9]{1,0:T(8,128)S(1)} %fusion.151, f32[9]{0:T(128)S(1)} %convolution_bitcast_fusion), channel_id=1, replica_groups=mesh['gx'=4,'gy'=4,'gz'=2] {'gx','gy','gz'}, use_global_device_ids=true, to_apply=%region_0.1 | all-reduce | flops 90 | bytes 720 | tf_op jit(solution)/shard_map/psum | solution.py:149
  (148 shorter events, 72.8 us)
Async XLA Ops:
  1.6 6.5 %collective-permute-start = (f32[2,3,10,130]{3,2,1,0:T(8,128)S(1)}, f32[2,3,10,130]{3,2,1,0:T(8,128)S(1)}, u32[]{:S(2)}, u32[]{:S(2)}) collective-permute-start(f32[2,3,10,130]{3,2,1,0:T(8,128)S(1)} %get-tuple-element.53), channel_id=1, source_target_pairs={{0,8},{8,16},{16,24},{1,9},{9,17},{17,25},{2,10},{10,18},{18,26},{... | collective-permute-start | bytes 93608 | tf_op jit(solution)/shard_map/ppermute | solution.py:20
  5.1 6.5 %collective-permute-start.1 = (f32[2,3,10,130]{3,2,1,0:T(8,128)S(1)}, f32[2,3,10,130]{3,2,1,0:T(8,128)S(1)}, u32[]{:S(2)}, u32[]{:S(2)}) collective-permute-start(f32[2,3,10,130]{3,2,1,0:T(8,128)S(1)} %get-tuple-element.54), channel_id=1, source_target_pairs={{8,0},{16,8},{24,16},{9,1},{17,9},{25,17},{10,2},{18,10},{26,18},{... | collective-permute-start | bytes 93608 | tf_op jit(solution)/shard_map/ppermute | solution.py:22
  11.6 6.3 %collective-permute-start.2 = (f32[2,16,3,130]{3,2,1,0:T(4,128)S(1)}, f32[2,16,3,130]{3,2,1,0:T(4,128)S(1)}, u32[]{:S(2)}, u32[]{:S(2)}) collective-permute-start(f32[2,16,3,130]{3,2,1,0:T(4,128)S(1)} %get-tuple-element.29), channel_id=1, source_target_pairs={{0,2},{2,4},{4,6},{1,3},{3,5},{5,7},{8,10},{10,12},{12,14},{9,11},... | collective-permute-start | bytes 149768 | tf_op jit(solution)/shard_map/ppermute | solution.py:20
  20.0 8.3 %collective-permute-start.4 = (f32[2,16,16,3]{3,2,1,0:T(8,128)S(1)}, f32[2,16,16,3]{3,2,1,0:T(8,128)S(1)}, u32[]{:S(2)}, u32[]{:S(2)}) collective-permute-start(f32[2,16,16,3]{3,2,1,0:T(8,128)S(1)} %get-tuple-element.27), channel_id=1, source_target_pairs={{0,1},{2,3},{4,5},{6,7},{8,9},{10,11},{12,13},{14,15},{16,17},{18,... | collective-permute-start | bytes 18440 | tf_op jit(solution)/shard_map/ppermute | solution.py:20
  21.3 8.4 %collective-permute-start.5 = (f32[2,16,16,3]{3,2,1,0:T(8,128)S(1)}, f32[2,16,16,3]{3,2,1,0:T(8,128)S(1)}, u32[]{:S(2)}, u32[]{:S(2)}) collective-permute-start(f32[2,16,16,3]{3,2,1,0:T(8,128)S(1)} %get-tuple-element.28), channel_id=1, source_target_pairs={{1,0},{3,2},{5,4},{7,6},{9,8},{11,10},{13,12},{15,14},{17,16},{19,... | collective-permute-start | bytes 18440 | tf_op jit(solution)/shard_map/ppermute | solution.py:22
  33.6 6.5 %collective-permute-start.6 = (f32[2,3,10,130]{3,2,1,0:T(8,128)S(1)}, f32[2,3,10,130]{3,2,1,0:T(8,128)S(1)}, u32[]{:S(2)}, u32[]{:S(2)}) collective-permute-start(f32[2,3,10,130]{3,2,1,0:T(8,128)S(1)} %get-tuple-element.51), channel_id=1, source_target_pairs={{0,8},{8,16},{16,24},{1,9},{9,17},{17,25},{2,10},{10,18},{18,26},{... | collective-permute-start | bytes 93608 | tf_op jit(solution)/shard_map/ppermute | solution.py:20
  37.1 6.5 %collective-permute-start.7 = (f32[2,3,10,130]{3,2,1,0:T(8,128)S(1)}, f32[2,3,10,130]{3,2,1,0:T(8,128)S(1)}, u32[]{:S(2)}, u32[]{:S(2)}) collective-permute-start(f32[2,3,10,130]{3,2,1,0:T(8,128)S(1)} %get-tuple-element.52), channel_id=1, source_target_pairs={{8,0},{16,8},{24,16},{9,1},{17,9},{25,17},{10,2},{18,10},{26,18},{... | collective-permute-start | bytes 93608 | tf_op jit(solution)/shard_map/ppermute | solution.py:22
  43.7 6.3 %collective-permute-start.8 = (f32[2,16,3,130]{3,2,1,0:T(4,128)S(1)}, f32[2,16,3,130]{3,2,1,0:T(4,128)S(1)}, u32[]{:S(2)}, u32[]{:S(2)}) collective-permute-start(f32[2,16,3,130]{3,2,1,0:T(4,128)S(1)} %get-tuple-element.25), channel_id=1, source_target_pairs={{0,2},{2,4},{4,6},{1,3},{3,5},{5,7},{8,10},{10,12},{12,14},{9,11},... | collective-permute-start | bytes 149768 | tf_op jit(solution)/shard_map/ppermute | solution.py:20
  52.0 8.3 %collective-permute-start.10 = (f32[2,16,16,3]{3,2,1,0:T(8,128)S(1)}, f32[2,16,16,3]{3,2,1,0:T(8,128)S(1)}, u32[]{:S(2)}, u32[]{:S(2)}) collective-permute-start(f32[2,16,16,3]{3,2,1,0:T(8,128)S(1)} %get-tuple-element.23), channel_id=1, source_target_pairs={{0,1},{2,3},{4,5},{6,7},{8,9},{10,11},{12,13},{14,15},{16,17},{18,... | collective-permute-start | bytes 18440 | tf_op jit(solution)/shard_map/ppermute | solution.py:20
  53.3 8.4 %collective-permute-start.11 = (f32[2,16,16,3]{3,2,1,0:T(8,128)S(1)}, f32[2,16,16,3]{3,2,1,0:T(8,128)S(1)}, u32[]{:S(2)}, u32[]{:S(2)}) collective-permute-start(f32[2,16,16,3]{3,2,1,0:T(8,128)S(1)} %get-tuple-element.24), channel_id=1, source_target_pairs={{1,0},{3,2},{5,4},{7,6},{9,8},{11,10},{13,12},{15,14},{17,16},{19,... | collective-permute-start | bytes 18440 | tf_op jit(solution)/shard_map/ppermute | solution.py:22
  64.3 6.5 %collective-permute-start.12 = (f32[2,3,10,130]{3,2,1,0:T(8,128)S(1)}, f32[2,3,10,130]{3,2,1,0:T(8,128)S(1)}, u32[]{:S(2)}, u32[]{:S(2)}) collective-permute-start(f32[2,3,10,130]{3,2,1,0:T(8,128)S(1)} %get-tuple-element.49), channel_id=1, source_target_pairs={{0,8},{8,16},{16,24},{1,9},{9,17},{17,25},{2,10},{10,18},{18,26},{... | collective-permute-start | bytes 93608 | tf_op jit(solution)/shard_map/ppermute | solution.py:20
  66.3 6.5 %collective-permute-start.13 = (f32[2,3,10,130]{3,2,1,0:T(8,128)S(1)}, f32[2,3,10,130]{3,2,1,0:T(8,128)S(1)}, u32[]{:S(2)}, u32[]{:S(2)}) collective-permute-start(f32[2,3,10,130]{3,2,1,0:T(8,128)S(1)} %get-tuple-element.50), channel_id=1, source_target_pairs={{8,0},{16,8},{24,16},{9,1},{17,9},{25,17},{10,2},{18,10},{26,18},{... | collective-permute-start | bytes 93608 | tf_op jit(solution)/shard_map/ppermute | solution.py:22
  72.8 6.3 %collective-permute-start.14 = (f32[2,16,3,130]{3,2,1,0:T(4,128)S(1)}, f32[2,16,3,130]{3,2,1,0:T(4,128)S(1)}, u32[]{:S(2)}, u32[]{:S(2)}) collective-permute-start(f32[2,16,3,130]{3,2,1,0:T(4,128)S(1)} %get-tuple-element.21), channel_id=1, source_target_pairs={{0,2},{2,4},{4,6},{1,3},{3,5},{5,7},{8,10},{10,12},{12,14},{9,11},... | collective-permute-start | bytes 149768 | tf_op jit(solution)/shard_map/ppermute | solution.py:20
  81.2 8.3 %collective-permute-start.16 = (f32[2,16,16,3]{3,2,1,0:T(8,128)S(1)}, f32[2,16,16,3]{3,2,1,0:T(8,128)S(1)}, u32[]{:S(2)}, u32[]{:S(2)}) collective-permute-start(f32[2,16,16,3]{3,2,1,0:T(8,128)S(1)} %get-tuple-element.19), channel_id=1, source_target_pairs={{0,1},{2,3},{4,5},{6,7},{8,9},{10,11},{12,13},{14,15},{16,17},{18,... | collective-permute-start | bytes 18440 | tf_op jit(solution)/shard_map/ppermute | solution.py:20
  82.5 8.4 %collective-permute-start.17 = (f32[2,16,16,3]{3,2,1,0:T(8,128)S(1)}, f32[2,16,16,3]{3,2,1,0:T(8,128)S(1)}, u32[]{:S(2)}, u32[]{:S(2)}) collective-permute-start(f32[2,16,16,3]{3,2,1,0:T(8,128)S(1)} %get-tuple-element.20), channel_id=1, source_target_pairs={{1,0},{3,2},{5,4},{7,6},{9,8},{11,10},{13,12},{15,14},{17,16},{19,... | collective-permute-start | bytes 18440 | tf_op jit(solution)/shard_map/ppermute | solution.py:22
  93.5 6.5 %collective-permute-start.18 = (f32[2,3,10,130]{3,2,1,0:T(8,128)S(1)}, f32[2,3,10,130]{3,2,1,0:T(8,128)S(1)}, u32[]{:S(2)}, u32[]{:S(2)}) collective-permute-start(f32[2,3,10,130]{3,2,1,0:T(8,128)S(1)} %get-tuple-element.47), channel_id=1, source_target_pairs={{0,8},{8,16},{16,24},{1,9},{9,17},{17,25},{2,10},{10,18},{18,26},{... | collective-permute-start | bytes 93608 | tf_op jit(solution)/shard_map/ppermute | solution.py:20
  95.4 6.5 %collective-permute-start.19 = (f32[2,3,10,130]{3,2,1,0:T(8,128)S(1)}, f32[2,3,10,130]{3,2,1,0:T(8,128)S(1)}, u32[]{:S(2)}, u32[]{:S(2)}) collective-permute-start(f32[2,3,10,130]{3,2,1,0:T(8,128)S(1)} %get-tuple-element.48), channel_id=1, source_target_pairs={{8,0},{16,8},{24,16},{9,1},{17,9},{25,17},{10,2},{18,10},{26,18},{... | collective-permute-start | bytes 93608 | tf_op jit(solution)/shard_map/ppermute | solution.py:22
  102.0 6.3 %collective-permute-start.20 = (f32[2,16,3,130]{3,2,1,0:T(4,128)S(1)}, f32[2,16,3,130]{3,2,1,0:T(4,128)S(1)}, u32[]{:S(2)}, u32[]{:S(2)}) collective-permute-start(f32[2,16,3,130]{3,2,1,0:T(4,128)S(1)} %get-tuple-element.17), channel_id=1, source_target_pairs={{0,2},{2,4},{4,6},{1,3},{3,5},{5,7},{8,10},{10,12},{12,14},{9,11},... | collective-permute-start | bytes 149768 | tf_op jit(solution)/shard_map/ppermute | solution.py:20
  110.3 8.3 %collective-permute-start.22 = (f32[2,16,16,3]{3,2,1,0:T(8,128)S(1)}, f32[2,16,16,3]{3,2,1,0:T(8,128)S(1)}, u32[]{:S(2)}, u32[]{:S(2)}) collective-permute-start(f32[2,16,16,3]{3,2,1,0:T(8,128)S(1)} %get-tuple-element.15), channel_id=1, source_target_pairs={{0,1},{2,3},{4,5},{6,7},{8,9},{10,11},{12,13},{14,15},{16,17},{18,... | collective-permute-start | bytes 18440 | tf_op jit(solution)/shard_map/ppermute | solution.py:20
  111.6 8.4 %collective-permute-start.23 = (f32[2,16,16,3]{3,2,1,0:T(8,128)S(1)}, f32[2,16,16,3]{3,2,1,0:T(8,128)S(1)}, u32[]{:S(2)}, u32[]{:S(2)}) collective-permute-start(f32[2,16,16,3]{3,2,1,0:T(8,128)S(1)} %get-tuple-element.16), channel_id=1, source_target_pairs={{1,0},{3,2},{5,4},{7,6},{9,8},{11,10},{13,12},{15,14},{17,16},{19,... | collective-permute-start | bytes 18440 | tf_op jit(solution)/shard_map/ppermute | solution.py:22
  122.7 6.5 %collective-permute-start.24 = (f32[2,3,10,130]{3,2,1,0:T(8,128)S(1)}, f32[2,3,10,130]{3,2,1,0:T(8,128)S(1)}, u32[]{:S(2)}, u32[]{:S(2)}) collective-permute-start(f32[2,3,10,130]{3,2,1,0:T(8,128)S(1)} %get-tuple-element.45), channel_id=1, source_target_pairs={{0,8},{8,16},{16,24},{1,9},{9,17},{17,25},{2,10},{10,18},{18,26},{... | collective-permute-start | bytes 93608 | tf_op jit(solution)/shard_map/ppermute | solution.py:20
  124.6 6.5 %collective-permute-start.25 = (f32[2,3,10,130]{3,2,1,0:T(8,128)S(1)}, f32[2,3,10,130]{3,2,1,0:T(8,128)S(1)}, u32[]{:S(2)}, u32[]{:S(2)}) collective-permute-start(f32[2,3,10,130]{3,2,1,0:T(8,128)S(1)} %get-tuple-element.46), channel_id=1, source_target_pairs={{8,0},{16,8},{24,16},{9,1},{17,9},{25,17},{10,2},{18,10},{26,18},{... | collective-permute-start | bytes 93608 | tf_op jit(solution)/shard_map/ppermute | solution.py:22
  139.5 8.3 %collective-permute-start.28 = (f32[2,16,16,3]{3,2,1,0:T(8,128)S(1)}, f32[2,16,16,3]{3,2,1,0:T(8,128)S(1)}, u32[]{:S(2)}, u32[]{:S(2)}) collective-permute-start(f32[2,16,16,3]{3,2,1,0:T(8,128)S(1)} %get-tuple-element.11), channel_id=1, source_target_pairs={{0,1},{2,3},{4,5},{6,7},{8,9},{10,11},{12,13},{14,15},{16,17},{18,... | collective-permute-start | bytes 18440 | tf_op jit(solution)/shard_map/ppermute | solution.py:20
  140.8 8.4 %collective-permute-start.29 = (f32[2,16,16,3]{3,2,1,0:T(8,128)S(1)}, f32[2,16,16,3]{3,2,1,0:T(8,128)S(1)}, u32[]{:S(2)}, u32[]{:S(2)}) collective-permute-start(f32[2,16,16,3]{3,2,1,0:T(8,128)S(1)} %get-tuple-element.12), channel_id=1, source_target_pairs={{1,0},{3,2},{5,4},{7,6},{9,8},{11,10},{13,12},{15,14},{17,16},{19,... | collective-permute-start | bytes 18440 | tf_op jit(solution)/shard_map/ppermute | solution.py:22
  (9 other events, 39.1 us)
where the time goes:
time: 199 us; the launch traced here: 198 us
  starting transfers between devices  86.5 us (43%)
  waiting for transfers between devices  46.7 us (23%)
  blocking collectives  42.5 us (21%)
  other arithmetic  13.6 us (7%)
  local copies, waits for them, and re-layouts  5.35 us (3%)
    ppermute x15, starting transfers between devices, extended(): lax.ppermute(head, axis, [((i + 1) % count, i) for i in range(ends)])  57.7 us
    psum x1, blocking collectives, local(): lax.psum((inner_table(basis_rows, image_rows), inner_vector(basis_rows, t...  42.5 us
    ppermute x15, waiting for transfers between devices, extended(): lax.ppermute(head, axis, [((i + 1) % count, i) for i in range(ends)])  29.1 us
    ppermute x15, starting transfers between devices, extended(): lax.ppermute(tail, axis, [(i, (i + 1) % count) for i in range(ends)])  28.8 us
    ppermute x15, waiting for transfers between devices, extended(): lax.ppermute(tail, axis, [(i, (i + 1) % count) for i in range(ends)])  17.6 us
  transfers between devices with their start and end apart: 30, of which 30 were waited for; matrix products, arithmetic and copies ran while one was open for 0% of the time, Pallas kernels for 0%

commit v1 on v0

--- a/solution.py
+++ b/solution.py
@@ -147,7 +147,10 @@
     basis_rows = flatten_rows(p_fields + z_fields)
     image_rows = flatten_rows(p_images + z_images)
     gram_sum, projection_sum = lax.psum(
-        (inner_table(basis_rows, image_rows), inner_vector(basis_rows, target)), ("gx", "gy", "gz")
+        lax.psum(
+            (inner_table(basis_rows, image_rows), inner_vector(basis_rows, target)), ("gy", "gz")
+        ),
+        "gx",
     )
     powers = jnp.stack([jnp.stack(p_fields[1:]), jnp.stack(z_fields)])
     return (powers, gram_sum / cell_count, projection_sum / cell_count)

time: 199 us -> 183 us (0.920)
  blocking collectives: 42.5 us -> 25.9 us
    psum x1, blocking collectives: 42.5 us -> 15.3 us  [local(): lax.psum((inner_table(basis_rows, image_rows), inner_vector(basis_rows, t...]
    psum x0 -> x1, blocking collectives: none -> 10.6 us  [local(): lax.psum(lax.psum((inner_table(basis_rows, image_rows), inner_vector(basi...]
where the time goes in v1:
time: 183 us; the launch traced here: 181 us
  starting transfers between devices  86.5 us (47%)
  waiting for transfers between devices  46.7 us (26%)
  blocking collectives  25.9 us (14%)
  other arithmetic  13.6 us (7%)
  local copies, waits for them, and re-layouts  5.35 us (3%)
    ppermute x15, starting transfers between devices, extended(): lax.ppermute(head, axis, [((i + 1) % count, i) for i in range(ends)])  57.7 us
    ppermute x15, waiting for transfers between devices, extended(): lax.ppermute(head, axis, [((i + 1) % count, i) for i in range(ends)])  29.1 us
    ppermute x15, starting transfers between devices, extended(): lax.ppermute(tail, axis, [(i, (i + 1) % count) for i in range(ends)])  28.8 us
    ppermute x15, waiting for transfers between devices, extended(): lax.ppermute(tail, axis, [(i, (i + 1) % count) for i in range(ends)])  17.6 us
    psum x1, blocking collectives, local(): lax.psum((inner_table(basis_rows, image_rows), inner_vector(basis_rows, t...  15.3 us
    psum x1, blocking collectives, local(): lax.psum(lax.psum((inner_table(basis_rows, image_rows), inner_vector(basi...  10.6 us
  transfers between devices with their start and end apart: 30, of which 30 were waited for; matrix products, arithmetic and copies ran while one was open for 0% of the time, Pallas kernels for 0%

profile of v1, /device:TPU:14, one launch (start us, length us, event | category | flops | bytes accessed | tf_op | source)
XLA Modules:
  0.0 181.0 jit_solution(13081775663867979381)
XLA Ops:
  1.6 3.5 %collective-permute-start = (f32[2,3,10,130]{3,2,1,0:T(8,128)S(1)}, f32[2,3,10,130]{3,2,1,0:T(8,128)S(1)}, u32[]{:S(2)}, u32[]{:S(2)}) collective-permute-start(f32[2,3,10,130]{3,2,1,0:T(8,128)S(1)} %get-tuple-element.55), channel_id=1, source_target_pairs={{0,8},{8,16},{16,24},{1,9},{9,17},{17,25},{2,10},{10,18},{18,26},{... | collective-permute-start | bytes 93608 | tf_op jit(solution)/shard_map/ppermute | solution.py:20
  5.1 2.4 %collective-permute-start.1 = (f32[2,3,10,130]{3,2,1,0:T(8,128)S(1)}, f32[2,3,10,130]{3,2,1,0:T(8,128)S(1)}, u32[]{:S(2)}, u32[]{:S(2)}) collective-permute-start(f32[2,3,10,130]{3,2,1,0:T(8,128)S(1)} %get-tuple-element.56), channel_id=1, source_target_pairs={{8,0},{16,8},{24,16},{9,1},{17,9},{25,17},{10,2},{18,10},{26,18},{... | collective-permute-start | bytes 93608 | tf_op jit(solution)/shard_map/ppermute | solution.py:22
  8.1 3.5 %collective-permute-done.1 = f32[2,3,10,130]{3,2,1,0:T(8,128)S(1)} collective-permute-done((f32[2,3,10,130]{3,2,1,0:T(8,128)S(1)}, f32[2,3,10,130]{3,2,1,0:T(8,128)S(1)}, u32[]{:S(2)}, u32[]{:S(2)}) %collective-permute-start.1) | collective-permute-done | bytes 31232 | tf_op jit(solution)/shard_map/ppermute | solution.py:22
  13.6 3.6 %collective-permute-start.3 = (f32[2,16,3,130]{3,2,1,0:T(4,128)S(1)}, f32[2,16,3,130]{3,2,1,0:T(4,128)S(1)}, u32[]{:S(2)}, u32[]{:S(2)}) collective-permute-start(f32[2,16,3,130]{3,2,1,0:T(4,128)S(1)} %get-tuple-element.32), channel_id=1, source_target_pairs={{2,0},{4,2},{6,4},{3,1},{5,3},{7,5},{10,8},{12,10},{14,12},{11,9},... | collective-permute-start | bytes 149768 | tf_op jit(solution)/shard_map/ppermute | solution.py:22
  21.3 4.6 %collective-permute-start.5 = (f32[2,16,16,3]{3,2,1,0:T(8,128)S(1)}, f32[2,16,16,3]{3,2,1,0:T(8,128)S(1)}, u32[]{:S(2)}, u32[]{:S(2)}) collective-permute-start(f32[2,16,16,3]{3,2,1,0:T(8,128)S(1)} %get-tuple-element.30), channel_id=1, source_target_pairs={{1,0},{3,2},{5,4},{7,6},{9,8},{11,10},{13,12},{15,14},{17,16},{19,... | collective-permute-start | bytes 18440 | tf_op jit(solution)/shard_map/ppermute | solution.py:22
  26.0 2.3 %collective-permute-done.4 = f32[2,16,16,3]{3,2,1,0:T(8,128)S(1)} collective-permute-done((f32[2,16,16,3]{3,2,1,0:T(8,128)S(1)}, f32[2,16,16,3]{3,2,1,0:T(8,128)S(1)}, u32[]{:S(2)}, u32[]{:S(2)}) %collective-permute-start.4) | collective-permute-done | bytes 6176 | tf_op jit(solution)/shard_map/ppermute | solution.py:20
  33.6 3.5 %collective-permute-start.6 = (f32[2,3,10,130]{3,2,1,0:T(8,128)S(1)}, f32[2,3,10,130]{3,2,1,0:T(8,128)S(1)}, u32[]{:S(2)}, u32[]{:S(2)}) collective-permute-start(f32[2,3,10,130]{3,2,1,0:T(8,128)S(1)} %get-tuple-element.53), channel_id=1, source_target_pairs={{0,8},{8,16},{16,24},{1,9},{9,17},{17,25},{2,10},{10,18},{18,26},{... | collective-permute-start | bytes 93608 | tf_op jit(solution)/shard_map/ppermute | solution.py:20
  37.1 2.4 %collective-permute-start.7 = (f32[2,3,10,130]{3,2,1,0:T(8,128)S(1)}, f32[2,3,10,130]{3,2,1,0:T(8,128)S(1)}, u32[]{:S(2)}, u32[]{:S(2)}) collective-permute-start(f32[2,3,10,130]{3,2,1,0:T(8,128)S(1)} %get-tuple-element.54), channel_id=1, source_target_pairs={{8,0},{16,8},{24,16},{9,1},{17,9},{25,17},{10,2},{18,10},{26,18},{... | collective-permute-start | bytes 93608 | tf_op jit(solution)/shard_map/ppermute | solution.py:22
  40.1 3.5 %collective-permute-done.7 = f32[2,3,10,130]{3,2,1,0:T(8,128)S(1)} collective-permute-done((f32[2,3,10,130]{3,2,1,0:T(8,128)S(1)}, f32[2,3,10,130]{3,2,1,0:T(8,128)S(1)}, u32[]{:S(2)}, u32[]{:S(2)}) %collective-permute-start.7) | collective-permute-done | bytes 31232 | tf_op jit(solution)/shard_map/ppermute | solution.py:22
  45.6 3.6 %collective-permute-start.9 = (f32[2,16,3,130]{3,2,1,0:T(4,128)S(1)}, f32[2,16,3,130]{3,2,1,0:T(4,128)S(1)}, u32[]{:S(2)}, u32[]{:S(2)}) collective-permute-start(f32[2,16,3,130]{3,2,1,0:T(4,128)S(1)} %get-tuple-element.28), channel_id=1, source_target_pairs={{2,0},{4,2},{6,4},{3,1},{5,3},{7,5},{10,8},{12,10},{14,12},{11,9},... | collective-permute-start | bytes 149768 | tf_op jit(solution)/shard_map/ppermute | solution.py:22
  53.3 4.6 %collective-permute-start.11 = (f32[2,16,16,3]{3,2,1,0:T(8,128)S(1)}, f32[2,16,16,3]{3,2,1,0:T(8,128)S(1)}, u32[]{:S(2)}, u32[]{:S(2)}) collective-permute-start(f32[2,16,16,3]{3,2,1,0:T(8,128)S(1)} %get-tuple-element.26), channel_id=1, source_target_pairs={{1,0},{3,2},{5,4},{7,6},{9,8},{11,10},{13,12},{15,14},{17,16},{19,... | collective-permute-start | bytes 18440 | tf_op jit(solution)/shard_map/ppermute | solution.py:22
  57.9 2.4 %collective-permute-done.10 = f32[2,16,16,3]{3,2,1,0:T(8,128)S(1)} collective-permute-done((f32[2,16,16,3]{3,2,1,0:T(8,128)S(1)}, f32[2,16,16,3]{3,2,1,0:T(8,128)S(1)}, u32[]{:S(2)}, u32[]{:S(2)}) %collective-permute-start.10) | collective-permute-done | bytes 6176 | tf_op jit(solution)/shard_map/ppermute | solution.py:20
  66.3 3.9 %collective-permute-start.13 = (f32[2,3,10,130]{3,2,1,0:T(8,128)S(1)}, f32[2,3,10,130]{3,2,1,0:T(8,128)S(1)}, u32[]{:S(2)}, u32[]{:S(2)}) collective-permute-start(f32[2,3,10,130]{3,2,1,0:T(8,128)S(1)} %get-tuple-element.52), channel_id=1, source_target_pairs={{8,0},{16,8},{24,16},{9,1},{17,9},{25,17},{10,2},{18,10},{26,18},{... | collective-permute-start | bytes 93608 | tf_op jit(solution)/shard_map/ppermute | solution.py:22
  74.8 3.6 %collective-permute-start.15 = (f32[2,16,3,130]{3,2,1,0:T(4,128)S(1)}, f32[2,16,3,130]{3,2,1,0:T(4,128)S(1)}, u32[]{:S(2)}, u32[]{:S(2)}) collective-permute-start(f32[2,16,3,130]{3,2,1,0:T(4,128)S(1)} %get-tuple-element.24), channel_id=1, source_target_pairs={{2,0},{4,2},{6,4},{3,1},{5,3},{7,5},{10,8},{12,10},{14,12},{11,9},... | collective-permute-start | bytes 149768 | tf_op jit(solution)/shard_map/ppermute | solution.py:22
  82.5 4.6 %collective-permute-start.17 = (f32[2,16,16,3]{3,2,1,0:T(8,128)S(1)}, f32[2,16,16,3]{3,2,1,0:T(8,128)S(1)}, u32[]{:S(2)}, u32[]{:S(2)}) collective-permute-start(f32[2,16,16,3]{3,2,1,0:T(8,128)S(1)} %get-tuple-element.22), channel_id=1, source_target_pairs={{1,0},{3,2},{5,4},{7,6},{9,8},{11,10},{13,12},{15,14},{17,16},{19,... | collective-permute-start | bytes 18440 | tf_op jit(solution)/shard_map/ppermute | solution.py:22
  95.4 3.9 %collective-permute-start.19 = (f32[2,3,10,130]{3,2,1,0:T(8,128)S(1)}, f32[2,3,10,130]{3,2,1,0:T(8,128)S(1)}, u32[]{:S(2)}, u32[]{:S(2)}) collective-permute-start(f32[2,3,10,130]{3,2,1,0:T(8,128)S(1)} %get-tuple-element.50), channel_id=1, source_target_pairs={{8,0},{16,8},{24,16},{9,1},{17,9},{25,17},{10,2},{18,10},{26,18},{... | collective-permute-start | bytes 93608 | tf_op jit(solution)/shard_map/ppermute | solution.py:22
  103.9 3.6 %collective-permute-start.21 = (f32[2,16,3,130]{3,2,1,0:T(4,128)S(1)}, f32[2,16,3,130]{3,2,1,0:T(4,128)S(1)}, u32[]{:S(2)}, u32[]{:S(2)}) collective-permute-start(f32[2,16,3,130]{3,2,1,0:T(4,128)S(1)} %get-tuple-element.20), channel_id=1, source_target_pairs={{2,0},{4,2},{6,4},{3,1},{5,3},{7,5},{10,8},{12,10},{14,12},{11,9},... | collective-permute-start | bytes 149768 | tf_op jit(solution)/shard_map/ppermute | solution.py:22
  111.6 4.8 %collective-permute-start.23 = (f32[2,16,16,3]{3,2,1,0:T(8,128)S(1)}, f32[2,16,16,3]{3,2,1,0:T(8,128)S(1)}, u32[]{:S(2)}, u32[]{:S(2)}) collective-permute-start(f32[2,16,16,3]{3,2,1,0:T(8,128)S(1)} %get-tuple-element.18), channel_id=1, source_target_pairs={{1,0},{3,2},{5,4},{7,6},{9,8},{11,10},{13,12},{15,14},{17,16},{19,... | collective-permute-start | bytes 18440 | tf_op jit(solution)/shard_map/ppermute | solution.py:22
  124.6 3.9 %collective-permute-start.25 = (f32[2,3,10,130]{3,2,1,0:T(8,128)S(1)}, f32[2,3,10,130]{3,2,1,0:T(8,128)S(1)}, u32[]{:S(2)}, u32[]{:S(2)}) collective-permute-start(f32[2,3,10,130]{3,2,1,0:T(8,128)S(1)} %get-tuple-element.48), channel_id=1, source_target_pairs={{8,0},{16,8},{24,16},{9,1},{17,9},{25,17},{10,2},{18,10},{26,18},{... | collective-permute-start | bytes 93608 | tf_op jit(solution)/shard_map/ppermute | solution.py:22
  133.1 3.6 %collective-permute-start.27 = (f32[2,16,3,130]{3,2,1,0:T(4,128)S(1)}, f32[2,16,3,130]{3,2,1,0:T(4,128)S(1)}, u32[]{:S(2)}, u32[]{:S(2)}) collective-permute-start(f32[2,16,3,130]{3,2,1,0:T(4,128)S(1)} %get-tuple-element.16), channel_id=1, source_target_pairs={{2,0},{4,2},{6,4},{3,1},{5,3},{7,5},{10,8},{12,10},{14,12},{11,9},... | collective-permute-start | bytes 149768 | tf_op jit(solution)/shard_map/ppermute | solution.py:22
  140.8 4.6 %collective-permute-start.29 = (f32[2,16,16,3]{3,2,1,0:T(8,128)S(1)}, f32[2,16,16,3]{3,2,1,0:T(8,128)S(1)}, u32[]{:S(2)}, u32[]{:S(2)}) collective-permute-start(f32[2,16,16,3]{3,2,1,0:T(8,128)S(1)} %get-tuple-element.14), channel_id=1, source_target_pairs={{1,0},{3,2},{5,4},{7,6},{9,8},{11,10},{13,12},{15,14},{17,16},{19,... | collective-permute-start | bytes 18440 | tf_op jit(solution)/shard_map/ppermute | solution.py:22
  145.5 2.3 %collective-permute-done.28 = f32[2,16,16,3]{3,2,1,0:T(8,128)S(1)} collective-permute-done((f32[2,16,16,3]{3,2,1,0:T(8,128)S(1)}, f32[2,16,16,3]{3,2,1,0:T(8,128)S(1)}, u32[]{:S(2)}, u32[]{:S(2)}) %collective-permute-start.28) | collective-permute-done | bytes 6176 | tf_op jit(solution)/shard_map/ppermute | solution.py:20
  153.3 15.3 %all-reduce.39 = (f32[9,9]{1,0:T(8,128)S(1)}, f32[9]{0:T(128)S(1)}) all-reduce(f32[9,9]{1,0:T(8,128)S(1)} %fusion.151, f32[9]{0:T(128)S(1)} %convolution_bitcast_fusion), channel_id=1, replica_groups=mesh['gx'=4,'gy'=4,'gz'=2] {'gy','gz'}, use_global_device_ids=true, to_apply=%region_0.1 | all-reduce | flops 90 | bytes 720 | tf_op jit(solution)/shard_map/psum | solution.py:150
  168.6 10.6 %all-reduce.40 = (f32[9,9]{1,0:T(8,128)S(1)}, f32[9]{0:T(128)S(1)}) all-reduce(f32[9,9]{1,0:T(8,128)S(1)} %get-tuple-element.3, f32[9]{0:T(128)S(1)} %get-tuple-element.4), channel_id=1, replica_groups=mesh['gx'=4,'gy'=4,'gz'=2] {'gx'}, use_global_device_ids=true, to_apply=%region_1.2 | all-reduce | flops 90 | bytes 720 | tf_op jit(solution)/shard_map/psum | solution.py:149
  (149 shorter events, 75.0 us)
Async XLA Ops:
  1.6 6.5 %collective-permute-start = (f32[2,3,10,130]{3,2,1,0:T(8,128)S(1)}, f32[2,3,10,130]{3,2,1,0:T(8,128)S(1)}, u32[]{:S(2)}, u32[]{:S(2)}) collective-permute-start(f32[2,3,10,130]{3,2,1,0:T(8,128)S(1)} %get-tuple-element.55), channel_id=1, source_target_pairs={{0,8},{8,16},{16,24},{1,9},{9,17},{17,25},{2,10},{10,18},{18,26},{... | collective-permute-start | bytes 93608 | tf_op jit(solution)/shard_map/ppermute | solution.py:20
  5.1 6.5 %collective-permute-start.1 = (f32[2,3,10,130]{3,2,1,0:T(8,128)S(1)}, f32[2,3,10,130]{3,2,1,0:T(8,128)S(1)}, u32[]{:S(2)}, u32[]{:S(2)}) collective-permute-start(f32[2,3,10,130]{3,2,1,0:T(8,128)S(1)} %get-tuple-element.56), channel_id=1, source_target_pairs={{8,0},{16,8},{24,16},{9,1},{17,9},{25,17},{10,2},{18,10},{26,18},{... | collective-permute-start | bytes 93608 | tf_op jit(solution)/shard_map/ppermute | solution.py:22
  11.6 6.3 %collective-permute-start.2 = (f32[2,16,3,130]{3,2,1,0:T(4,128)S(1)}, f32[2,16,3,130]{3,2,1,0:T(4,128)S(1)}, u32[]{:S(2)}, u32[]{:S(2)}) collective-permute-start(f32[2,16,3,130]{3,2,1,0:T(4,128)S(1)} %get-tuple-element.31), channel_id=1, source_target_pairs={{0,2},{2,4},{4,6},{1,3},{3,5},{5,7},{8,10},{10,12},{12,14},{9,11},... | collective-permute-start | bytes 149768 | tf_op jit(solution)/shard_map/ppermute | solution.py:20
  20.0 8.3 %collective-permute-start.4 = (f32[2,16,16,3]{3,2,1,0:T(8,128)S(1)}, f32[2,16,16,3]{3,2,1,0:T(8,128)S(1)}, u32[]{:S(2)}, u32[]{:S(2)}) collective-permute-start(f32[2,16,16,3]{3,2,1,0:T(8,128)S(1)} %get-tuple-element.29), channel_id=1, source_target_pairs={{0,1},{2,3},{4,5},{6,7},{8,9},{10,11},{12,13},{14,15},{16,17},{18,... | collective-permute-start | bytes 18440 | tf_op jit(solution)/shard_map/ppermute | solution.py:20
  21.3 8.4 %collective-permute-start.5 = (f32[2,16,16,3]{3,2,1,0:T(8,128)S(1)}, f32[2,16,16,3]{3,2,1,0:T(8,128)S(1)}, u32[]{:S(2)}, u32[]{:S(2)}) collective-permute-start(f32[2,16,16,3]{3,2,1,0:T(8,128)S(1)} %get-tuple-element.30), channel_id=1, source_target_pairs={{1,0},{3,2},{5,4},{7,6},{9,8},{11,10},{13,12},{15,14},{17,16},{19,... | collective-permute-start | bytes 18440 | tf_op jit(solution)/shard_map/ppermute | solution.py:22
  33.6 6.5 %collective-permute-start.6 = (f32[2,3,10,130]{3,2,1,0:T(8,128)S(1)}, f32[2,3,10,130]{3,2,1,0:T(8,128)S(1)}, u32[]{:S(2)}, u32[]{:S(2)}) collective-permute-start(f32[2,3,10,130]{3,2,1,0:T(8,128)S(1)} %get-tuple-element.53), channel_id=1, source_target_pairs={{0,8},{8,16},{16,24},{1,9},{9,17},{17,25},{2,10},{10,18},{18,26},{... | collective-permute-start | bytes 93608 | tf_op jit(solution)/shard_map/ppermute | solution.py:20
  37.1 6.5 %collective-permute-start.7 = (f32[2,3,10,130]{3,2,1,0:T(8,128)S(1)}, f32[2,3,10,130]{3,2,1,0:T(8,128)S(1)}, u32[]{:S(2)}, u32[]{:S(2)}) collective-permute-start(f32[2,3,10,130]{3,2,1,0:T(8,128)S(1)} %get-tuple-element.54), channel_id=1, source_target_pairs={{8,0},{16,8},{24,16},{9,1},{17,9},{25,17},{10,2},{18,10},{26,18},{... | collective-permute-start | bytes 93608 | tf_op jit(solution)/shard_map/ppermute | solution.py:22
  43.7 6.3 %collective-permute-start.8 = (f32[2,16,3,130]{3,2,1,0:T(4,128)S(1)}, f32[2,16,3,130]{3,2,1,0:T(4,128)S(1)}, u32[]{:S(2)}, u32[]{:S(2)}) collective-permute-start(f32[2,16,3,130]{3,2,1,0:T(4,128)S(1)} %get-tuple-element.27), channel_id=1, source_target_pairs={{0,2},{2,4},{4,6},{1,3},{3,5},{5,7},{8,10},{10,12},{12,14},{9,11},... | collective-permute-start | bytes 149768 | tf_op jit(solution)/shard_map/ppermute | solution.py:20
  52.0 8.3 %collective-permute-start.10 = (f32[2,16,16,3]{3,2,1,0:T(8,128)S(1)}, f32[2,16,16,3]{3,2,1,0:T(8,128)S(1)}, u32[]{:S(2)}, u32[]{:S(2)}) collective-permute-start(f32[2,16,16,3]{3,2,1,0:T(8,128)S(1)} %get-tuple-element.25), channel_id=1, source_target_pairs={{0,1},{2,3},{4,5},{6,7},{8,9},{10,11},{12,13},{14,15},{16,17},{18,... | collective-permute-start | bytes 18440 | tf_op jit(solution)/shard_map/ppermute | solution.py:20
  53.3 8.4 %collective-permute-start.11 = (f32[2,16,16,3]{3,2,1,0:T(8,128)S(1)}, f32[2,16,16,3]{3,2,1,0:T(8,128)S(1)}, u32[]{:S(2)}, u32[]{:S(2)}) collective-permute-start(f32[2,16,16,3]{3,2,1,0:T(8,128)S(1)} %get-tuple-element.26), channel_id=1, source_target_pairs={{1,0},{3,2},{5,4},{7,6},{9,8},{11,10},{13,12},{15,14},{17,16},{19,... | collective-permute-start | bytes 18440 | tf_op jit(solution)/shard_map/ppermute | solution.py:22
  64.3 6.5 %collective-permute-start.12 = (f32[2,3,10,130]{3,2,1,0:T(8,128)S(1)}, f32[2,3,10,130]{3,2,1,0:T(8,128)S(1)}, u32[]{:S(2)}, u32[]{:S(2)}) collective-permute-start(f32[2,3,10,130]{3,2,1,0:T(8,128)S(1)} %get-tuple-element.51), channel_id=1, source_target_pairs={{0,8},{8,16},{16,24},{1,9},{9,17},{17,25},{2,10},{10,18},{18,26},{... | collective-permute-start | bytes 93608 | tf_op jit(solution)/shard_map/ppermute | solution.py:20
  66.3 6.5 %collective-permute-start.13 = (f32[2,3,10,130]{3,2,1,0:T(8,128)S(1)}, f32[2,3,10,130]{3,2,1,0:T(8,128)S(1)}, u32[]{:S(2)}, u32[]{:S(2)}) collective-permute-start(f32[2,3,10,130]{3,2,1,0:T(8,128)S(1)} %get-tuple-element.52), channel_id=1, source_target_pairs={{8,0},{16,8},{24,16},{9,1},{17,9},{25,17},{10,2},{18,10},{26,18},{... | collective-permute-start | bytes 93608 | tf_op jit(solution)/shard_map/ppermute | solution.py:22
  72.8 6.3 %collective-permute-start.14 = (f32[2,16,3,130]{3,2,1,0:T(4,128)S(1)}, f32[2,16,3,130]{3,2,1,0:T(4,128)S(1)}, u32[]{:S(2)}, u32[]{:S(2)}) collective-permute-start(f32[2,16,3,130]{3,2,1,0:T(4,128)S(1)} %get-tuple-element.23), channel_id=1, source_target_pairs={{0,2},{2,4},{4,6},{1,3},{3,5},{5,7},{8,10},{10,12},{12,14},{9,11},... | collective-permute-start | bytes 149768 | tf_op jit(solution)/shard_map/ppermute | solution.py:20
  81.2 8.3 %collective-permute-start.16 = (f32[2,16,16,3]{3,2,1,0:T(8,128)S(1)}, f32[2,16,16,3]{3,2,1,0:T(8,128)S(1)}, u32[]{:S(2)}, u32[]{:S(2)}) collective-permute-start(f32[2,16,16,3]{3,2,1,0:T(8,128)S(1)} %get-tuple-element.21), channel_id=1, source_target_pairs={{0,1},{2,3},{4,5},{6,7},{8,9},{10,11},{12,13},{14,15},{16,17},{18,... | collective-permute-start | bytes 18440 | tf_op jit(solution)/shard_map/ppermute | solution.py:20
  82.5 8.4 %collective-permute-start.17 = (f32[2,16,16,3]{3,2,1,0:T(8,128)S(1)}, f32[2,16,16,3]{3,2,1,0:T(8,128)S(1)}, u32[]{:S(2)}, u32[]{:S(2)}) collective-permute-start(f32[2,16,16,3]{3,2,1,0:T(8,128)S(1)} %get-tuple-element.22), channel_id=1, source_target_pairs={{1,0},{3,2},{5,4},{7,6},{9,8},{11,10},{13,12},{15,14},{17,16},{19,... | collective-permute-start | bytes 18440 | tf_op jit(solution)/shard_map/ppermute | solution.py:22
  93.5 6.5 %collective-permute-start.18 = (f32[2,3,10,130]{3,2,1,0:T(8,128)S(1)}, f32[2,3,10,130]{3,2,1,0:T(8,128)S(1)}, u32[]{:S(2)}, u32[]{:S(2)}) collective-permute-start(f32[2,3,10,130]{3,2,1,0:T(8,128)S(1)} %get-tuple-element.49), channel_id=1, source_target_pairs={{0,8},{8,16},{16,24},{1,9},{9,17},{17,25},{2,10},{10,18},{18,26},{... | collective-permute-start | bytes 93608 | tf_op jit(solution)/shard_map/ppermute | solution.py:20
  95.4 6.5 %collective-permute-start.19 = (f32[2,3,10,130]{3,2,1,0:T(8,128)S(1)}, f32[2,3,10,130]{3,2,1,0:T(8,128)S(1)}, u32[]{:S(2)}, u32[]{:S(2)}) collective-permute-start(f32[2,3,10,130]{3,2,1,0:T(8,128)S(1)} %get-tuple-element.50), channel_id=1, source_target_pairs={{8,0},{16,8},{24,16},{9,1},{17,9},{25,17},{10,2},{18,10},{26,18},{... | collective-permute-start | bytes 93608 | tf_op jit(solution)/shard_map/ppermute | solution.py:22
  102.0 6.3 %collective-permute-start.20 = (f32[2,16,3,130]{3,2,1,0:T(4,128)S(1)}, f32[2,16,3,130]{3,2,1,0:T(4,128)S(1)}, u32[]{:S(2)}, u32[]{:S(2)}) collective-permute-start(f32[2,16,3,130]{3,2,1,0:T(4,128)S(1)} %get-tuple-element.19), channel_id=1, source_target_pairs={{0,2},{2,4},{4,6},{1,3},{3,5},{5,7},{8,10},{10,12},{12,14},{9,11},... | collective-permute-start | bytes 149768 | tf_op jit(solution)/shard_map/ppermute | solution.py:20
  110.3 8.3 %collective-permute-start.22 = (f32[2,16,16,3]{3,2,1,0:T(8,128)S(1)}, f32[2,16,16,3]{3,2,1,0:T(8,128)S(1)}, u32[]{:S(2)}, u32[]{:S(2)}) collective-permute-start(f32[2,16,16,3]{3,2,1,0:T(8,128)S(1)} %get-tuple-element.17), channel_id=1, source_target_pairs={{0,1},{2,3},{4,5},{6,7},{8,9},{10,11},{12,13},{14,15},{16,17},{18,... | collective-permute-start | bytes 18440 | tf_op jit(solution)/shard_map/ppermute | solution.py:20
  111.6 8.4 %collective-permute-start.23 = (f32[2,16,16,3]{3,2,1,0:T(8,128)S(1)}, f32[2,16,16,3]{3,2,1,0:T(8,128)S(1)}, u32[]{:S(2)}, u32[]{:S(2)}) collective-permute-start(f32[2,16,16,3]{3,2,1,0:T(8,128)S(1)} %get-tuple-element.18), channel_id=1, source_target_pairs={{1,0},{3,2},{5,4},{7,6},{9,8},{11,10},{13,12},{15,14},{17,16},{19,... | collective-permute-start | bytes 18440 | tf_op jit(solution)/shard_map/ppermute | solution.py:22
  122.7 6.5 %collective-permute-start.24 = (f32[2,3,10,130]{3,2,1,0:T(8,128)S(1)}, f32[2,3,10,130]{3,2,1,0:T(8,128)S(1)}, u32[]{:S(2)}, u32[]{:S(2)}) collective-permute-start(f32[2,3,10,130]{3,2,1,0:T(8,128)S(1)} %get-tuple-element.47), channel_id=1, source_target_pairs={{0,8},{8,16},{16,24},{1,9},{9,17},{17,25},{2,10},{10,18},{18,26},{... | collective-permute-start | bytes 93608 | tf_op jit(solution)/shard_map/ppermute | solution.py:20
  124.6 6.5 %collective-permute-start.25 = (f32[2,3,10,130]{3,2,1,0:T(8,128)S(1)}, f32[2,3,10,130]{3,2,1,0:T(8,128)S(1)}, u32[]{:S(2)}, u32[]{:S(2)}) collective-permute-start(f32[2,3,10,130]{3,2,1,0:T(8,128)S(1)} %get-tuple-element.48), channel_id=1, source_target_pairs={{8,0},{16,8},{24,16},{9,1},{17,9},{25,17},{10,2},{18,10},{26,18},{... | collective-permute-start | bytes 93608 | tf_op jit(solution)/shard_map/ppermute | solution.py:22
  139.5 8.3 %collective-permute-start.28 = (f32[2,16,16,3]{3,2,1,0:T(8,128)S(1)}, f32[2,16,16,3]{3,2,1,0:T(8,128)S(1)}, u32[]{:S(2)}, u32[]{:S(2)}) collective-permute-start(f32[2,16,16,3]{3,2,1,0:T(8,128)S(1)} %get-tuple-element.13), channel_id=1, source_target_pairs={{0,1},{2,3},{4,5},{6,7},{8,9},{10,11},{12,13},{14,15},{16,17},{18,... | collective-permute-start | bytes 18440 | tf_op jit(solution)/shard_map/ppermute | solution.py:20
  140.8 8.4 %collective-permute-start.29 = (f32[2,16,16,3]{3,2,1,0:T(8,128)S(1)}, f32[2,16,16,3]{3,2,1,0:T(8,128)S(1)}, u32[]{:S(2)}, u32[]{:S(2)}) collective-permute-start(f32[2,16,16,3]{3,2,1,0:T(8,128)S(1)} %get-tuple-element.14), channel_id=1, source_target_pairs={{1,0},{3,2},{5,4},{7,6},{9,8},{11,10},{13,12},{15,14},{17,16},{19,... | collective-permute-start | bytes 18440 | tf_op jit(solution)/shard_map/ppermute | solution.py:22
  (9 other events, 39.1 us)
